TPU v7x, 8 devices: a whole 2x2x1 slice. The times are simulated.
8 devices in a mesh: dp: 1 (over z), col: 2 (over y), row: 4 (over x, core).
Axes of the slice: x: 2, y: 2, z: 1, core: 2. Of those that a mesh axis runs over, the one named last changes fastest.
Arguments:
- latent: bfloat16 [16, 16, 96, 384], P('dp', 'row', 'col')
- t_emb: bfloat16 [16, 768], P('dp')
- res_norm: bfloat16 [2, 2, 2, 384], replicated
- res_conv: bfloat16 [2, 2, 3, 3, 384, 384], replicated
- res_temb: bfloat16 [2, 768, 384], replicated
- attn_norm: bfloat16 [2, 384], replicated
- attn_proj: bfloat16 [4, 12, 384, 32], replicated
Outputs:
- output: bfloat16 [16, 16, 96, 384], P('dp', 'row', 'col')
All inputs are finite; a program needn't handle non-finite values.
Results may differ from a plain program's by a relative error of at most 0.00941283.
Values are sent between devices in bfloat16 or wider.
A program may use at most 1 GiB of HBM per device.

v0:
```python
import jax
import jax.numpy as jnp
from jax import lax
from jax.sharding import PartitionSpec as P

GROUPS = 32
EPS = 1e-5


def group_norm(values, gn_scale, gn_shift, n_dev):
    n_batch, n_rows, n_cols, n_chan = values.shape
    group_ch = n_chan // GROUPS
    grouped = values.astype(jnp.float32).reshape(n_batch, n_rows, n_cols, GROUPS, group_ch)
    part_sums = jnp.stack([jnp.sum(grouped, axis=(1, 2, 4)), jnp.sum(grouped * grouped, axis=(1, 2, 4))])
    moments = lax.psum(part_sums, ('row', 'col')) / (n_rows * n_cols * group_ch * n_dev)
    mean_val = moments[0]
    inv_std = lax.rsqrt(moments[1] - mean_val * mean_val + EPS)
    normed = (grouped - mean_val[:, None, None, :, None]) * inv_std[:, None, None, :, None]
    return normed.reshape(values.shape) * gn_scale.astype(jnp.float32) + gn_shift.astype(jnp.float32)


def halo_conv(acts_in, kernel, n_row, n_col):
    to_next_row = [(i, i + 1) for i in range(n_row - 1)]
    to_prev_row = [(i + 1, i) for i in range(n_row - 1)]
    to_next_col = [(i, i + 1) for i in range(n_col - 1)]
    to_prev_col = [(i + 1, i) for i in range(n_col - 1)]
    from_above = lax.ppermute(acts_in[:, -1:], 'row', to_next_row)
    from_below = lax.ppermute(acts_in[:, :1], 'row', to_prev_row)
    row_padded = jnp.concatenate([from_above, acts_in, from_below], axis=1)
    from_left = lax.ppermute(row_padded[:, :, -1:], 'col', to_next_col)
    from_right = lax.ppermute(row_padded[:, :, :1], 'col', to_prev_col)
    padded = jnp.concatenate([from_left, row_padded, from_right], axis=2)
    return lax.conv_general_dilated(padded, kernel, (1, 1), 'VALID', dimension_numbers=('NHWC', 'HWIO', 'NHWC'), preferred_element_type=jnp.float32)


def res_block(latent, t_emb, norm_par, kernels, w_temb, n_row, n_col):
    n_dev = n_row * n_col
    t_act = jax.nn.silu(t_emb.astype(jnp.float32)).astype(jnp.bfloat16)
    t_proj = jnp.dot(t_act, w_temb, preferred_element_type=jnp.float32)
    first_act = jax.nn.silu(group_norm(latent, norm_par[0, 0], norm_par[0, 1], n_dev)).astype(jnp.bfloat16)
    hidden = (halo_conv(first_act, kernels[0], n_row, n_col) + t_proj[:, None, None, :]).astype(jnp.bfloat16)
    second_act = jax.nn.silu(group_norm(hidden, norm_par[1, 0], norm_par[1, 1], n_dev)).astype(jnp.bfloat16)
    return (latent.astype(jnp.float32) + halo_conv(second_act, kernels[1], n_row, n_col)).astype(jnp.bfloat16)


def attend(queries, keys_all, values_all, n_blocks):
    n_batch, n_query, n_heads, head_dim = queries.shape
    blk_len = keys_all.shape[1] // n_blocks
    key_blocks = keys_all.reshape(n_batch, n_blocks, blk_len, n_heads, head_dim)
    val_blocks = values_all.reshape(n_batch, n_blocks, blk_len, n_heads, head_dim)
    inv_scale = head_dim ** -0.5

    def key_step(blk_idx, loop_state):
        run_max, run_sum, out_acc = loop_state
        key_blk = lax.dynamic_index_in_dim(key_blocks, blk_idx, axis=1, keepdims=False)
        val_blk = lax.dynamic_index_in_dim(val_blocks, blk_idx, axis=1, keepdims=False)
        logits = jnp.einsum('bqhd,bkhd->bhqk', queries, key_blk, preferred_element_type=jnp.float32) * inv_scale
        new_max = jnp.maximum(run_max, jnp.max(logits, axis=-1))
        rescale = jnp.exp(run_max - new_max)
        exp_logits = jnp.exp(logits - new_max[..., None])
        run_sum = run_sum * rescale + jnp.sum(exp_logits, axis=-1)
        out_acc = out_acc * rescale[..., None] + jnp.einsum('bhqk,bkhd->bhqd', exp_logits.astype(jnp.bfloat16), val_blk, preferred_element_type=jnp.float32)
        return new_max, run_sum, out_acc

    carry_init = (jnp.full((n_batch, n_heads, n_query), -jnp.inf, jnp.float32), jnp.zeros((n_batch, n_heads, n_query), jnp.float32), jnp.zeros((n_batch, n_heads, n_query, head_dim), jnp.float32))
    run_max, run_sum, out_acc = lax.fori_loop(0, n_blocks, key_step, carry_init)
    return out_acc / run_sum[..., None]


def attn_block(latent, norm_par, proj_w, n_dev):
    n_batch, n_rows, n_cols, n_chan = latent.shape
    normed = group_norm(latent, norm_par[0], norm_par[1], n_dev).astype(jnp.bfloat16).reshape(n_batch, n_rows * n_cols, n_chan)
    qkv_loc = jnp.einsum('bnc,khcd->kbnhd', normed, proj_w[:3], preferred_element_type=jnp.float32).astype(jnp.bfloat16)
    kv_all = lax.all_gather(qkv_loc[1:], ('row', 'col'), axis=2, tiled=True)
    attn_out = attend(qkv_loc[0], kv_all[0], kv_all[1], n_dev).astype(jnp.bfloat16)
    out_proj = jnp.einsum('bhqd,hcd->bqc', attn_out, proj_w[3], preferred_element_type=jnp.float32)
    return (latent.astype(jnp.float32) + out_proj.reshape(latent.shape)).astype(jnp.bfloat16)


def solution(mesh):
    n_row = mesh.shape['row']
    n_col = mesh.shape['col']

    def run_stage(latent, t_emb, res_norm, res_conv, res_temb, attn_norm, attn_proj):
        hidden = res_block(latent, t_emb, res_norm[0], res_conv[0], res_temb[0], n_row, n_col)
        hidden = attn_block(hidden, attn_norm, attn_proj, n_row * n_col)
        return res_block(hidden, t_emb, res_norm[1], res_conv[1], res_temb[1], n_row, n_col)

    spec_x = P('dp', 'row', 'col', None)
    return jax.shard_map(run_stage, mesh=mesh, in_specs=(spec_x, P('dp', None), P(), P(), P(), P(), P()), out_specs=spec_x, check_vma=False)
```

profile of v0, /device:TPU:1, one launch (start us, length us, event | category | flops | bytes accessed | tf_op | source)
XLA Modules:
  0.0 1688.9 jit_solution(15304578632372645981)
XLA Ops:
  10.4 23.3 %psum.35 = f32[2,16,32]{2,1,0:T(8,128)S(1)} all-reduce(f32[2,16,32]{2,1,0:T(8,128)S(1)} %pad_maximum_fusion.12), channel_id=1, replica_groups=mesh['dp'=1,'col'=2,'row'=4] {'row','col'}, use_global_device_ids=true, to_apply=%region_4.5 | all-reduce | flops 1024 | bytes 8192 | tf_op jit(solution)/shard_map/psum | solution.py:15
  38.1 5.3 collective-permute-start
  45.3 4.9 collective-permute-done
  50.2 4.7 collective-permute-done.1
  58.4 3.6 collective-permute-done.3
  61.9 14.7 convert_reduce_fusion.4
  77.5 20.8 %psum.36 = f32[2,16,32]{2,1,0:T(8,128)S(1)} all-reduce(f32[2,16,32]{2,1,0:T(8,128)S(1)} %pad_maximum_fusion.13), channel_id=1, replica_groups=mesh['dp'=1,'col'=2,'row'=4] {'row','col'}, use_global_device_ids=true, to_apply=%region_9.10 | all-reduce | flops 1024 | bytes 8192 | tf_op jit(solution)/shard_map/psum | solution.py:15
  99.0 3.3 fusion.30
  102.4 5.2 collective-permute-start.4
  109.5 4.9 collective-permute-done.4
  114.4 4.4 collective-permute-done.5
  118.8 3.7 collective-permute-start.6
  123.9 3.7 collective-permute-done.7
  127.6 17.2 %convert_reduce_fusion.1 = (f32[16,384]{1,0:T(8,128)S(1)}, f32[16,384]{1,0:T(8,128)S(1)}, bf16[16,4,48,384]{3,0,2,1:T(8,128)(2,1)}) fusion(bf16[2,2,3,3,384,384]{5,4,3,2,1,0:T(8,128)(2,1)} %param.12, bf16[16,6,1,384]{3,0,2,1:T(8,128)(2,1)S(1)} %collective-permute-done.7, bf16[16,1,48,384]{3,0,2,1:T(8,128)(2,1)S(1)} %collective-permute-done.5, ...), kind=kOutput, calls=%fused_computation.30 | convolution fusion | flops 8169345024 | bytes 11108352 | tf_op jit(solution)/shard_map/conv_general_dilated | solution.py:33
  145.7 21.0 %psum.37 = f32[2,16,32]{2,1,0:T(8,128)S(1)} all-reduce(f32[2,16,32]{2,1,0:T(8,128)S(1)} %pad_maximum_fusion.14), channel_id=1, replica_groups=mesh['dp'=1,'col'=2,'row'=4] {'row','col'}, use_global_device_ids=true, to_apply=%region_14.15 | all-reduce | flops 1024 | bytes 8192 | tf_op jit(solution)/shard_map/psum | solution.py:15
  169.9 5.4 convert_bitcast_fusion
  175.3 3.6 copy-done.1
  178.9 3.4 slice.224
  182.3 16.8 copy.27
  201.6 653.7 %all-gather.2.cloned.1.call-done = bf16[2,16,1536,12,32]{4,1,3,0,2:T(8,128)(2,1)} async-done(((bf16[2,16,192,12,32]{4,1,3,0,2:T(8,128)(2,1)}), bf16[2,16,1536,12,32]{4,1,3,0,2:T(8,128)(2,1)}) %all-gather.2.cloned.1.call-update) | async-done | bytes 37748752 | tf_op jit(solution)/shard_map/all_gather | solution.py:74
  855.3 97.5 %fusion.178 = (bf16[1,16,1536,12,32]{4,1,3,0,2:T(8,128)(2,1)}, bf16[1,16,1536,12,32]{4,1,3,0,2:T(8,128)(2,1)}) fusion(bf16[2,16,1536,12,32]{4,1,3,0,2:T(8,128)(2,1)} %all-gather.2.cloned.1.call-done), kind=kLoop, calls=%fused_computation.230 | loop fusion | bytes 75497472 | tf_op jit(solution)/shard_map/slice | solution.py:75
  952.9 71.4 %copy.28 = bf16[16,8,192,12,32]{2,4,3,0,1:T(8,128)(2,1)} copy(bf16[16,8,192,12,32]{4,0,3,2,1:T(8,128)(2,1)} %bitcast.20) | data formatting | bytes 37748736
  1024.3 71.4 %copy.29 = bf16[16,8,192,12,32]{2,4,3,0,1:T(8,128)(2,1)} copy(bf16[16,8,192,12,32]{4,0,3,2,1:T(8,128)(2,1)} %bitcast.22) | data formatting | bytes 37748736
  1095.6 437.0 %while.18 = (s32[]{:T(128)}, f32[16,12,192]{2,1,0:T(8,128)}, f32[16,12,192]{2,1,0:T(8,128)}, f32[16,12,192,32]{2,3,1,0:T(8,128)}, bf16[16,8,192,12,32]{2,4,3,0,1...) while((s32[]{:T(128)}, f32[16,12,192]{2,1,0:T(8,128)}, ...), condition=%wide.region_18.19_spmd.clone, body=%wide.region_15.18_spmd.clone.sunk | while | flops 966316032 | bytes 118162616 | solution.py:66
  1095.8 16.2 bitcast_reduce_fusion.2
  1112.1 16.7 fusion.194
  1129.0 18.3 %fusion.196 = f32[16,12,192,32]{2,3,1,0:T(8,128)} fusion(f32[16,12,192,32]{2,3,1,0:T(8,128)} %get-tuple-element.306, f32[16,12,192]{2,1,0:T(8,128)S(1)} %get-tuple-element.293, pred[]{:T(512)S(6)} %compare.3, f32[16,12,192,192]{3,2,1,0:T(8,128)} %get-tuple-element.291, f32[16,12,192]{2,1,0:T(8,128)S(1)} %select_maximum_fusion.2, ...), kind=kOutput, calls=%fused_computation.9.clone.1 | convolution fusion | flops 477757440 | bytes 52199936 | tf_op jit(solution)/shard_map/while/body/eval_jaxpr/bhqk,bkhd->bhqd/dot_general | solution.py:62
  1148.0 16.2 bitcast_reduce_fusion.2
  1165.2 16.7 fusion.194
  1182.2 20.1 %fusion.196 = f32[16,12,192,32]{2,3,1,0:T(8,128)} fusion(f32[16,12,192,32]{2,3,1,0:T(8,128)} %get-tuple-element.306, f32[16,12,192]{2,1,0:T(8,128)S(1)} %get-tuple-element.293, pred[]{:T(512)S(6)} %compare.3, f32[16,12,192,192]{3,2,1,0:T(8,128)} %get-tuple-element.291, f32[16,12,192]{2,1,0:T(8,128)S(1)} %select_maximum_fusion.2, ...), kind=kOutput, calls=%fused_computation.9.clone.1 | convolution fusion | flops 477757440 | bytes 52199936 | tf_op jit(solution)/shard_map/while/body/eval_jaxpr/bhqk,bkhd->bhqd/dot_general | solution.py:62
  1203.0 16.2 bitcast_reduce_fusion.2
  1220.2 16.7 fusion.194
  1237.1 20.1 %fusion.196 = f32[16,12,192,32]{2,3,1,0:T(8,128)} fusion(f32[16,12,192,32]{2,3,1,0:T(8,128)} %get-tuple-element.306, f32[16,12,192]{2,1,0:T(8,128)S(1)} %get-tuple-element.293, pred[]{:T(512)S(6)} %compare.3, f32[16,12,192,192]{3,2,1,0:T(8,128)} %get-tuple-element.291, f32[16,12,192]{2,1,0:T(8,128)S(1)} %select_maximum_fusion.2, ...), kind=kOutput, calls=%fused_computation.9.clone.1 | convolution fusion | flops 477757440 | bytes 52199936 | tf_op jit(solution)/shard_map/while/body/eval_jaxpr/bhqk,bkhd->bhqd/dot_general | solution.py:62
  1257.9 16.2 bitcast_reduce_fusion.2
  1275.1 16.7 fusion.194
  1292.1 20.1 %fusion.196 = f32[16,12,192,32]{2,3,1,0:T(8,128)} fusion(f32[16,12,192,32]{2,3,1,0:T(8,128)} %get-tuple-element.306, f32[16,12,192]{2,1,0:T(8,128)S(1)} %get-tuple-element.293, pred[]{:T(512)S(6)} %compare.3, f32[16,12,192,192]{3,2,1,0:T(8,128)} %get-tuple-element.291, f32[16,12,192]{2,1,0:T(8,128)S(1)} %select_maximum_fusion.2, ...), kind=kOutput, calls=%fused_computation.9.clone.1 | convolution fusion | flops 477757440 | bytes 52199936 | tf_op jit(solution)/shard_map/while/body/eval_jaxpr/bhqk,bkhd->bhqd/dot_general | solution.py:62
  1312.9 16.2 bitcast_reduce_fusion.2
  1330.1 16.7 fusion.194
  1347.0 20.1 %fusion.196 = f32[16,12,192,32]{2,3,1,0:T(8,128)} fusion(f32[16,12,192,32]{2,3,1,0:T(8,128)} %get-tuple-element.306, f32[16,12,192]{2,1,0:T(8,128)S(1)} %get-tuple-element.293, pred[]{:T(512)S(6)} %compare.3, f32[16,12,192,192]{3,2,1,0:T(8,128)} %get-tuple-element.291, f32[16,12,192]{2,1,0:T(8,128)S(1)} %select_maximum_fusion.2, ...), kind=kOutput, calls=%fused_computation.9.clone.1 | convolution fusion | flops 477757440 | bytes 52199936 | tf_op jit(solution)/shard_map/while/body/eval_jaxpr/bhqk,bkhd->bhqd/dot_general | solution.py:62
  1367.8 16.2 bitcast_reduce_fusion.2
  1385.0 16.7 fusion.194
  1402.0 20.1 %fusion.196 = f32[16,12,192,32]{2,3,1,0:T(8,128)} fusion(f32[16,12,192,32]{2,3,1,0:T(8,128)} %get-tuple-element.306, f32[16,12,192]{2,1,0:T(8,128)S(1)} %get-tuple-element.293, pred[]{:T(512)S(6)} %compare.3, f32[16,12,192,192]{3,2,1,0:T(8,128)} %get-tuple-element.291, f32[16,12,192]{2,1,0:T(8,128)S(1)} %select_maximum_fusion.2, ...), kind=kOutput, calls=%fused_computation.9.clone.1 | convolution fusion | flops 477757440 | bytes 52199936 | tf_op jit(solution)/shard_map/while/body/eval_jaxpr/bhqk,bkhd->bhqd/dot_general | solution.py:62
  1422.8 16.2 bitcast_reduce_fusion.2
  1440.0 16.7 fusion.194
  1456.9 20.1 %fusion.196 = f32[16,12,192,32]{2,3,1,0:T(8,128)} fusion(f32[16,12,192,32]{2,3,1,0:T(8,128)} %get-tuple-element.306, f32[16,12,192]{2,1,0:T(8,128)S(1)} %get-tuple-element.293, pred[]{:T(512)S(6)} %compare.3, f32[16,12,192,192]{3,2,1,0:T(8,128)} %get-tuple-element.291, f32[16,12,192]{2,1,0:T(8,128)S(1)} %select_maximum_fusion.2, ...), kind=kOutput, calls=%fused_computation.9.clone.1 | convolution fusion | flops 477757440 | bytes 52199936 | tf_op jit(solution)/shard_map/while/body/eval_jaxpr/bhqk,bkhd->bhqd/dot_general | solution.py:62
  1477.7 16.2 bitcast_reduce_fusion.2
  1494.9 16.7 fusion.194
  1511.9 20.1 %fusion.196 = f32[16,12,192,32]{2,3,1,0:T(8,128)} fusion(f32[16,12,192,32]{2,3,1,0:T(8,128)} %get-tuple-element.306, f32[16,12,192]{2,1,0:T(8,128)S(1)} %get-tuple-element.293, pred[]{:T(512)S(6)} %compare.3, f32[16,12,192,192]{3,2,1,0:T(8,128)} %get-tuple-element.291, f32[16,12,192]{2,1,0:T(8,128)S(1)} %select_maximum_fusion.2, ...), kind=kOutput, calls=%fused_computation.9.clone.1 | convolution fusion | flops 477757440 | bytes 52199936 | tf_op jit(solution)/shard_map/while/body/eval_jaxpr/bhqk,bkhd->bhqd/dot_general | solution.py:62
  1532.7 3.9 fusion.109
  1536.6 7.3 copy.42
  1543.8 7.2 convert_reduce_fusion
  1551.9 21.3 %psum.38 = f32[2,16,32]{2,1,0:T(8,128)S(1)} all-reduce(f32[2,16,32]{2,1,0:T(8,128)S(1)} %pad_maximum_fusion.15), channel_id=1, replica_groups=mesh['dp'=1,'col'=2,'row'=4] {'row','col'}, use_global_device_ids=true, to_apply=%region_23.24 | all-reduce | flops 1024 | bytes 8192 | tf_op jit(solution)/shard_map/psum | solution.py:15
  1575.7 5.3 collective-permute-start.8
  1582.9 4.9 collective-permute-done.8
  1587.8 4.4 collective-permute-done.9
  1596.9 3.6 collective-permute-done.11
  1600.5 14.7 convert_reduce_fusion.3
  1616.0 20.9 %psum.39 = f32[2,16,32]{2,1,0:T(8,128)S(1)} all-reduce(f32[2,16,32]{2,1,0:T(8,128)S(1)} %pad_maximum_fusion.16), channel_id=1, replica_groups=mesh['dp'=1,'col'=2,'row'=4] {'row','col'}, use_global_device_ids=true, to_apply=%region_28.29 | all-reduce | flops 1024 | bytes 8192 | tf_op jit(solution)/shard_map/psum | solution.py:15
  1641.0 5.2 collective-permute-start.12
  1648.1 4.9 collective-permute-done.12
  1653.0 4.4 collective-permute-done.13
  1657.4 3.7 collective-permute-start.14
  1662.5 3.7 collective-permute-done.15
  1666.2 13.4 fusion.68
  (194 shorter events, 58.8 us)
Async XLA Ops:
  6.5 29.2 %copy-start.2 = (bf16[16,4,48,384]{3,2,1,0:T(8,128)(2,1)S(1)}, bf16[16,4,48,384]{3,2,1,0:T(8,128)(2,1)}, u32[]{:S(2)}) copy-start(bf16[16,4,48,384]{3,2,1,0:T(8,128)(2,1)} %param.9) | copy-start | bytes 7077892
  6.5 848.8 %all-gather.2.cloned.1.call-start = ((), (), s32[]{:S(2)}) async-start(), calls=%async_computation | async-start | bytes 169869312 | tf_op jit(solution)/shard_map/all_gather | solution.py:74
  35.8 22.4 %copy-start.11 = (bf16[2,768,384]{2,1,0:T(8,128)(2,1)S(1)}, bf16[2,768,384]{2,1,0:T(8,128)(2,1)}, u32[]{:S(2)}) copy-start(bf16[2,768,384]{2,1,0:T(8,128)(2,1)} %param.13) | copy-start | bytes 3538948
  35.8 22.4 %copy-start.13 = (bf16[16,768]{1,0:T(8,128)(2,1)S(1)}, bf16[16,768]{1,0:T(8,128)(2,1)}, u32[]{:S(2)}) copy-start(bf16[16,768]{1,0:T(8,128)(2,1)} %param.10) | copy-start | bytes 73732
  38.1 12.0 collective-permute-start
  43.4 11.5 collective-permute-start.1
  54.9 3.4 collective-permute-start.2
  56.8 5.1 collective-permute-start.3
  99.0 24.8 %copy-start.9 = (bf16[2,384]{1,0:T(2,128)(2,1)S(1)}, bf16[2,384]{1,0:T(2,128)(2,1)}, u32[]{:S(2)}) copy-start(bf16[2,384]{1,0:T(2,128)(2,1)} %param.14) | copy-start | bytes 4612
  102.4 11.9 collective-permute-start.4
  107.6 11.2 collective-permute-start.5
  118.8 5.1 collective-permute-start.6
  122.5 5.1 collective-permute-start.7
  144.9 25.1 %copy-start.10 = (bf16[4,12,384,32]{2,3,1,0:T(8,128)(2,1)S(1)}, bf16[4,12,384,32]{2,3,1,0:T(8,128)(2,1)}, u32[]{:S(2)}) copy-start(bf16[4,12,384,32]{2,3,1,0:T(8,128)(2,1)} %param.15) | copy-start | bytes 3538948
  175.3 3.6 copy-start.1
  1112.1 16.7 copy-start
  1112.1 16.7 copy-start.3
  1129.0 18.3 %copy-start.4 = (f32[16,12,192]{2,1,0:T(8,128)}, f32[16,12,192]{2,1,0:T(8,128)S(1)}, u32[]{:S(2)}) copy-start(f32[16,12,192]{2,1,0:T(8,128)S(1)} %get-tuple-element.314) | copy-start | bytes 442372 | tf_op jit(solution)/shard_map/while
  1165.2 16.7 copy-start
  1165.2 16.7 copy-start.3
  1182.2 20.1 %copy-start.4 = (f32[16,12,192]{2,1,0:T(8,128)}, f32[16,12,192]{2,1,0:T(8,128)S(1)}, u32[]{:S(2)}) copy-start(f32[16,12,192]{2,1,0:T(8,128)S(1)} %get-tuple-element.314) | copy-start | bytes 442372 | tf_op jit(solution)/shard_map/while
  1220.2 16.7 copy-start
  1220.2 16.7 copy-start.3
  1237.1 20.1 %copy-start.4 = (f32[16,12,192]{2,1,0:T(8,128)}, f32[16,12,192]{2,1,0:T(8,128)S(1)}, u32[]{:S(2)}) copy-start(f32[16,12,192]{2,1,0:T(8,128)S(1)} %get-tuple-element.314) | copy-start | bytes 442372 | tf_op jit(solution)/shard_map/while
  1275.1 16.7 copy-start
  1275.1 16.7 copy-start.3
  1292.1 20.1 %copy-start.4 = (f32[16,12,192]{2,1,0:T(8,128)}, f32[16,12,192]{2,1,0:T(8,128)S(1)}, u32[]{:S(2)}) copy-start(f32[16,12,192]{2,1,0:T(8,128)S(1)} %get-tuple-element.314) | copy-start | bytes 442372 | tf_op jit(solution)/shard_map/while
  1330.1 16.7 copy-start
  1330.1 16.7 copy-start.3
  1347.0 20.1 %copy-start.4 = (f32[16,12,192]{2,1,0:T(8,128)}, f32[16,12,192]{2,1,0:T(8,128)S(1)}, u32[]{:S(2)}) copy-start(f32[16,12,192]{2,1,0:T(8,128)S(1)} %get-tuple-element.314) | copy-start | bytes 442372 | tf_op jit(solution)/shard_map/while
  1385.0 16.7 copy-start
  1385.0 16.7 copy-start.3
  1402.0 20.1 %copy-start.4 = (f32[16,12,192]{2,1,0:T(8,128)}, f32[16,12,192]{2,1,0:T(8,128)S(1)}, u32[]{:S(2)}) copy-start(f32[16,12,192]{2,1,0:T(8,128)S(1)} %get-tuple-element.314) | copy-start | bytes 442372 | tf_op jit(solution)/shard_map/while
  1439.9 16.7 copy-start
  1440.0 16.7 copy-start.3
  1456.9 20.1 %copy-start.4 = (f32[16,12,192]{2,1,0:T(8,128)}, f32[16,12,192]{2,1,0:T(8,128)S(1)}, u32[]{:S(2)}) copy-start(f32[16,12,192]{2,1,0:T(8,128)S(1)} %get-tuple-element.314) | copy-start | bytes 442372 | tf_op jit(solution)/shard_map/while
  1494.9 16.7 copy-start
  1494.9 16.7 copy-start.3
  1511.8 20.1 %copy-start.4 = (f32[16,12,192]{2,1,0:T(8,128)}, f32[16,12,192]{2,1,0:T(8,128)S(1)}, u32[]{:S(2)}) copy-start(f32[16,12,192]{2,1,0:T(8,128)S(1)} %get-tuple-element.314) | copy-start | bytes 442372 | tf_op jit(solution)/shard_map/while
  1543.8 30.1 %copy-start.7 = (f32[384]{0:T(512)S(1)}, f32[384]{0:T(512)}, u32[]{:S(2)}) copy-start(f32[384]{0:T(512)} %get-tuple-element.189) | copy-start | bytes 4612
  1543.8 30.1 %copy-start.8 = (f32[384]{0:T(512)S(1)}, f32[384]{0:T(512)}, u32[]{:S(2)}) copy-start(f32[384]{0:T(512)} %get-tuple-element.190) | copy-start | bytes 4612
  1573.9 22.7 %copy-start.12 = (bf16[2,768,384]{2,1,0:T(8,128)(2,1)S(1)}, bf16[2,768,384]{2,1,0:T(8,128)(2,1)}, u32[]{:S(2)}) copy-start(bf16[2,768,384]{2,1,0:T(8,128)(2,1)} %param.13) | copy-start | bytes 3538948
  1573.9 22.7 %copy-start.14 = (bf16[16,768]{1,0:T(8,128)(2,1)S(1)}, bf16[16,768]{1,0:T(8,128)(2,1)}, u32[]{:S(2)}) copy-start(bf16[16,768]{1,0:T(8,128)(2,1)} %param.10) | copy-start | bytes 73732
  1575.7 12.0 collective-permute-start.8
  1581.0 11.2 collective-permute-start.9
  1592.2 4.7 collective-permute-start.10
  1595.4 5.1 collective-permute-start.11
  1596.9 40.7 %copy-start.5 = (f32[384]{0:T(512)S(1)}, f32[384]{0:T(512)}, u32[]{:S(2)}) copy-start(f32[384]{0:T(512)} %get-tuple-element.187) | copy-start | bytes 4612
  1596.9 40.7 %copy-start.6 = (f32[384]{0:T(512)S(1)}, f32[384]{0:T(512)}, u32[]{:S(2)}) copy-start(f32[384]{0:T(512)} %get-tuple-element.188) | copy-start | bytes 4612
  1641.0 11.9 collective-permute-start.12
  1646.2 11.2 collective-permute-start.13
  1657.4 5.1 collective-permute-start.14
  1661.1 5.1 collective-permute-start.15
Sparse Core Ops, SparseCore 0:
  199.3 655.9 all-gather.1
where the time goes:
time: 1700 us; the launch traced here: 1690 us
  waiting for transfers between devices  706 us (42%)
  matrix products  362 us (21%)
  local copies, waits for them, and re-layouts  288 us (17%)
  other arithmetic  164 us (10%)
  blocking collectives  107 us (6%)
  starting transfers between devices  46 us (3%)
    all_gather x1, waiting for transfers between devices, attn_block(): kv_all = lax.all_gather(qkv_loc[1:], ('row', 'col'), axis=2, tiled=True)  654 us
    dot_general x8, matrix products, key_step(): jnp.einsum('bhqk,bkhd->bhqd', exp_logits.astype(jnp.bfloat16), val_blk, p...  159 us
    unnamed x26, local copies, waits for them, and re-layouts  146 us
    reduce_sum x8, other arithmetic, key_step(): run_sum = run_sum * rescale + jnp.sum(exp_logits, axis=-1)  134 us
    dot_general x8, matrix products, key_step(): jnp.einsum('bqhd,bkhd->bhqk', queries, key_blk, preferred_element_type=jn...  130 us
    psum x5, blocking collectives, group_norm(): lax.psum(part_sums, ('row', 'col')) / (n_rows * n_cols * group_ch * n_dev)  107 us
    slice x1, local copies, waits for them, and re-layouts, attn_block(): kv_all[1]  97.5 us
    conv_general_dilated x4, matrix products, halo_conv(): lax.conv_general_dilated(padded, kernel, (1, 1), 'VALID', dimension_numbe...  60.2 us
  transfers between devices with their start and end apart: 17, of which 15 were waited for; matrix products, arithmetic and copies ran while one was open for 0% of the time, Pallas kernels for 0%

commit v1 on v0

v1 whole, which is shorter than its diff:
```python
import functools

import jax
import jax.numpy as jnp
from jax import lax
from jax.experimental import pallas as pl
from jax.experimental.pallas import tpu as pltpu
from jax.sharding import PartitionSpec as P

MESH = pl.DeviceIdType.MESH
GROUPS = 32
EPS = 1e-5
LOG2E = 1.4426950408889634
F32 = jnp.float32
BF16 = jnp.bfloat16
Q_TILE = 256
ROWS_PER_CHUNK = 4


def _peers(n_row, n_col):
    me_r, me_c = lax.axis_index('row'), lax.axis_index('col')
    out = []
    for k in range(1, n_row * n_col):
        r = lax.rem(me_r + k // n_col, n_row)
        c = lax.rem(me_c + k % n_col, n_col)
        out.append((r, c))
    return me_r, me_c, out


def _barrier(peers):
    sem = pltpu.get_barrier_semaphore()
    for r, c in peers:
        pl.semaphore_signal(sem, inc=1, device_id={'row': r, 'col': c}, device_id_type=MESH)
    pl.semaphore_wait(sem, len(peers))


def _gather_kernel(n_row, n_col, x_ref, o_ref, send_sem, recv_sem, loc_sem):
    me_r, me_c, peers = _peers(n_row, n_col)
    n_img, bh, bw = o_ref.shape[0], x_ref.shape[1], x_ref.shape[2]
    place = o_ref.at[:, pl.ds(me_r * bh, bh), pl.ds(pl.multiple_of(me_c * bw, bw), bw), :]
    _barrier(peers)
    copies = []
    for k, (r, c) in enumerate(peers):
        dst = r * n_col + c
        copies.append(pltpu.make_async_remote_copy(
            x_ref.at[pl.ds(dst * n_img, n_img)], place, send_sem.at[k], recv_sem.at[k],
            device_id={'row': r, 'col': c}, device_id_type=MESH))
    for cp in copies:
        cp.start()
    me = me_r * n_col + me_c
    loc = pltpu.make_async_copy(x_ref.at[pl.ds(me * n_img, n_img)], place, loc_sem)
    loc.start()
    for cp in copies:
        cp.wait()
    loc.wait()


def _scatter_kernel(n_row, n_col, y_ref, o_ref, send_sem, recv_sem, loc_sem):
    me_r, me_c, peers = _peers(n_row, n_col)
    n_img, bh, bw = y_ref.shape[0], o_ref.shape[1], o_ref.shape[2]
    me = me_r * n_col + me_c
    place = o_ref.at[pl.ds(me * n_img, n_img)]

    def block(r, c):
        return y_ref.at[:, pl.ds(r * bh, bh), pl.ds(pl.multiple_of(c * bw, bw), bw), :]

    _barrier(peers)
    copies = []
    for k, (r, c) in enumerate(peers):
        copies.append(pltpu.make_async_remote_copy(
            block(r, c), place, send_sem.at[k], recv_sem.at[k],
            device_id={'row': r, 'col': c}, device_id_type=MESH))
    for cp in copies:
        cp.start()
    loc = pltpu.make_async_copy(block(me_r, me_c), place, loc_sem)
    loc.start()
    for cp in copies:
        cp.wait()
    loc.wait()


def _exchange(kernel, arr, out_shape, n_dev, cid):
    return pl.pallas_call(
        kernel,
        out_shape=jax.ShapeDtypeStruct(out_shape, arr.dtype),
        in_specs=[pl.BlockSpec(memory_space=pl.ANY)],
        out_specs=pl.BlockSpec(memory_space=pl.ANY),
        scratch_shapes=[
            pltpu.SemaphoreType.DMA((n_dev - 1,)),
            pltpu.SemaphoreType.DMA((n_dev - 1,)),
            pltpu.SemaphoreType.DMA,
        ],
        compiler_params=pltpu.CompilerParams(collective_id=cid, has_side_effects=True),
    )(arr)


def _dot(a, b, dims=((1,), (0,))):
    return lax.dot_general(a, b, (dims, ((), ())), preferred_element_type=F32)


def _stage_kernel(n_col, hh, ww, x_ref, temb_ref, rnorm_ref, conv_hbm, wtemb_ref, anorm_ref, proj_ref,
                  o_ref, wconv, act, hid, res, temb_s, g_buf, k_buf, q_buf, v_buf, ot_buf, grp_s, sem):
    img = pl.program_id(0)
    n_pos, n_ch = hh * ww, x_ref.shape[-1]
    n_imgs = pl.num_programs(0)
    count = float(n_pos * (n_ch // GROUPS))
    chunk = ROWS_PER_CHUNK * ww
    n_chunks = n_pos // chunk
    me = lax.axis_index('row') * n_col + lax.axis_index('col')

    def weight_copy(i):
        return pltpu.make_async_copy(conv_hbm.at[i // 2, i % 2], wconv.at[i], sem.at[i])

    @pl.when(img == 0)
    def _():
        for i in range(4):
            weight_copy(i).start()
        te = temb_ref[...].astype(F32)
        t_act = (te * jax.nn.sigmoid(te)).astype(BF16)
        for r in range(2):
            temb_s[r] = _dot(t_act, wtemb_ref[r])
        per = n_ch // GROUPS
        gi = lax.broadcasted_iota(jnp.int32, (n_ch, n_ch), 0) // per
        gj = lax.broadcasted_iota(jnp.int32, (n_ch, n_ch), 1) // per
        grp_s[...] = jnp.where(gi == gj, 1.0, 0.0).astype(BF16)
        zeros = jnp.zeros((ww, act.shape[1]), BF16)
        act[0:ww, :] = zeros
        act[(hh + 1) * ww:(hh + 2) * ww, :] = zeros

    def moments(s1, s2):
        st = jnp.concatenate([s1, s2, jnp.zeros((6, n_ch), F32)], axis=0)
        hi = st.astype(BF16)
        r1 = st - hi.astype(F32)
        mid = r1.astype(BF16)
        lo = (r1 - mid.astype(F32)).astype(BF16)
        grp = grp_s[...]
        tot = (_dot(lo, grp) + _dot(mid, grp)) + _dot(hi, grp)
        mean = tot[0:1] / count
        var = tot[1:2] / count - mean * mean
        return mean, lax.rsqrt(var + EPS)

    def chan_sums(v):
        return jnp.sum(v, axis=0, keepdims=True), jnp.sum(v * v, axis=0, keepdims=True)

    zero_sums = (jnp.zeros((1, n_ch), F32), jnp.zeros((1, n_ch), F32))

    def fill_act(src, mean, inv, scale, shift):
        a_mul = inv * scale.astype(F32)
        b_add = shift.astype(F32)
        col = lax.broadcasted_iota(jnp.int32, (ww, 1), 0)

        def row(i, carry):
            r0 = pl.multiple_of(i * ww, ww)
            v = src(r0, ww).astype(F32)
            u = (v - mean) * a_mul + b_add
            a = u * (0.5 * jnp.tanh(0.5 * u) + 0.5)
            left = jnp.where(col == 0, 0.0, pltpu.roll(a, 1, 0))
            right = jnp.where(col == ww - 1, 0.0, pltpu.roll(a, ww - 1, 0))
            d0 = pl.multiple_of(r0 + ww, ww)
            act[pl.ds(d0, ww), 0:n_ch] = left.astype(BF16)
            act[pl.ds(d0, ww), n_ch:2 * n_ch] = a.astype(BF16)
            act[pl.ds(d0, ww), 2 * n_ch:3 * n_ch] = right.astype(BF16)
            return carry

        lax.fori_loop(0, hh, row, 0)

    def conv(w_idx, epilogue):
        @pl.when(img == 0)
        def _():
            weight_copy(w_idx).wait()

        def body(i, sums):
            r0 = pl.multiple_of(i * chunk, chunk)
            lhs = jnp.concatenate([act[pl.ds(pl.multiple_of(r0 + dy * ww, ww), chunk), :] for dy in range(3)], axis=1)
            out = epilogue(r0, _dot(lhs, wconv[w_idx]))
            d1, d2 = chan_sums(out.astype(F32))
            return sums[0] + d1, sums[1] + d2

        return lax.fori_loop(0, n_chunks, body, zero_sums, unroll=2)

    def res_block(r, src, sums, dst):
        mean, inv = moments(*sums)
        fill_act(src, mean, inv, rnorm_ref[r, 0, 0:1], rnorm_ref[r, 0, 1:2])
        t_row = temb_s[r, pl.ds(me * n_imgs + img, 1), :]

        def first(r0, acc):
            out = (acc + t_row).astype(BF16)
            hid[pl.ds(r0, chunk), :] = out
            return out

        sums = conv(2 * r, first)
        mean, inv = moments(*sums)
        fill_act(lambda r0, n: hid[pl.ds(r0, n), :], mean, inv, rnorm_ref[r, 1, 0:1], rnorm_ref[r, 1, 1:2])

        def second(r0, acc):
            out = (src(r0, chunk).astype(F32) + acc).astype(BF16)
            dst(r0, out)
            return out

        return conv(2 * r + 1, second)

    def read_x(r0, n):
        return x_ref[0, pl.ds(r0, n), :]

    def read_res(r0, n):
        return res[pl.ds(r0, n), :]

    def write_res(r0, v):
        res[pl.ds(r0, chunk), :] = v

    def write_out(r0, v):
        o_ref[0, pl.ds(r0, chunk), :] = v

    def x_sums(i, sums):
        d1, d2 = chan_sums(read_x(pl.multiple_of(i * chunk, chunk), chunk).astype(F32))
        return sums[0] + d1, sums[1] + d2

    sums = lax.fori_loop(0, n_chunks, x_sums, zero_sums)
    sums = res_block(0, read_x, sums, write_res)

    mean, inv = moments(*sums)
    a_mul = inv * anorm_ref[0:1].astype(F32)
    b_add = anorm_ref[1:2].astype(F32)

    def project(i, carry):
        r0 = pl.multiple_of(i * Q_TILE, Q_TILE)
        g = ((read_res(r0, Q_TILE).astype(F32) - mean) * a_mul + b_add).astype(BF16)
        q_buf[:, pl.ds(r0, Q_TILE)] = _dot(proj_ref[0], g, ((1,), (1,))).astype(BF16)
        v_buf[:, pl.ds(r0, Q_TILE)] = _dot(proj_ref[2], g, ((1,), (1,))).astype(BF16)
        k_buf[pl.ds(r0, Q_TILE), :] = _dot(g, proj_ref[1], ((1,), (1,))).astype(BF16)
        return carry

    lax.fori_loop(0, n_pos // Q_TILE, project, 0)

    head_dim = 32
    n_heads = n_ch // head_dim
    per_blk = 128 // head_dim
    n_tiles = n_pos // Q_TILE
    scale = LOG2E * head_dim ** -0.5
    row_head = lax.broadcasted_iota(jnp.int32, (128, Q_TILE), 0) // head_dim

    def attend(i, carry):
        h = i // n_tiles
        q0 = pl.multiple_of((i % n_tiles) * Q_TILE, Q_TILE)
        b0 = pl.multiple_of((h // per_blk) * 128, 128)
        h0 = pl.multiple_of(h * head_dim, head_dim)
        qm = jnp.where(row_head == h % per_blk, q_buf[pl.ds(b0, 128), pl.ds(q0, Q_TILE)], 0)
        s = _dot(k_buf[:, pl.ds(b0, 128)], qm)
        m = jnp.max(s, axis=0, keepdims=True)
        p = jnp.exp2((s - m) * scale)
        l = jnp.sum(p, axis=0, keepdims=True)
        o = _dot(v_buf[pl.ds(h0, head_dim), :], p.astype(BF16))
        ot_buf[pl.ds(h0, head_dim), pl.ds(q0, Q_TILE)] = (o / l).astype(BF16)
        return carry

    lax.fori_loop(0, n_heads * n_tiles, attend, 0)

    def out_proj(i, sums):
        r0 = pl.multiple_of(i * chunk, chunk)
        acc = _dot(ot_buf[:, pl.ds(r0, chunk)], proj_ref[3], ((0,), (0,)))
        out = (read_res(r0, chunk).astype(F32) + acc).astype(BF16)
        write_res(r0, out)
        d1, d2 = chan_sums(out.astype(F32))
        return sums[0] + d1, sums[1] + d2

    sums = lax.fori_loop(0, n_chunks, out_proj, zero_sums)
    res_block(1, read_res, sums, write_out)


def _stage(images, hh, ww, n_col, t_emb, res_norm, res_conv, res_temb, attn_norm, attn_proj):
    n_img, n_pos, n_ch = images.shape
    proj = jnp.transpose(attn_proj, (0, 1, 3, 2)).reshape(4, n_ch, n_ch)
    conv_w = res_conv.reshape(2, 2, 9 * n_ch, n_ch)

    def whole(a):
        return pl.BlockSpec(a.shape, lambda i, nd=a.ndim: (0,) * nd, pipeline_mode=pl.Buffered(1))

    img_spec = pl.BlockSpec((1, n_pos, n_ch), lambda i: (i, 0, 0))
    return pl.pallas_call(
        functools.partial(_stage_kernel, n_col, hh, ww),
        grid=(n_img,),
        out_shape=jax.ShapeDtypeStruct(images.shape, BF16),
        in_specs=[img_spec, whole(t_emb), whole(res_norm), pl.BlockSpec(memory_space=pl.ANY), whole(res_temb),
                  whole(attn_norm), whole(proj)],
        out_specs=img_spec,
        scratch_shapes=[
            pltpu.VMEM((4, 9 * n_ch, n_ch), BF16),
            pltpu.VMEM(((hh + 2) * ww, 3 * n_ch), BF16),
            pltpu.VMEM((n_pos, n_ch), BF16),
            pltpu.VMEM((n_pos, n_ch), BF16),
            pltpu.VMEM((2, t_emb.shape[0], n_ch), F32),
            pltpu.VMEM((8, n_ch), BF16),
            pltpu.VMEM((n_pos, n_ch), BF16),
            pltpu.VMEM((n_ch, n_pos), BF16),
            pltpu.VMEM((n_ch, n_pos), BF16),
            pltpu.VMEM((n_ch, n_pos), BF16),
            pltpu.VMEM((n_ch, n_ch), BF16),
            pltpu.SemaphoreType.DMA((4,)),
        ],
        compiler_params=pltpu.CompilerParams(dimension_semantics=("arbitrary",), vmem_limit_bytes=60 * 1024 * 1024),
    )(images, t_emb, res_norm, conv_w, res_temb, attn_norm, proj)


def solution(mesh):
    n_row, n_col = mesh.shape['row'], mesh.shape['col']
    n_dev = n_row * n_col

    def run_stage(latent, t_emb, res_norm, res_conv, res_temb, attn_norm, attn_proj):
        n_batch, bh, bw, n_ch = latent.shape
        hh, ww = bh * n_row, bw * n_col
        n_img = n_batch // n_dev
        images = _exchange(functools.partial(_gather_kernel, n_row, n_col), latent, (n_img, hh, ww, n_ch), n_dev, 0)
        out = _stage(images.reshape(n_img, hh * ww, n_ch), hh, ww, n_col, t_emb, res_norm, res_conv, res_temb,
                     attn_norm, attn_proj)
        return _exchange(functools.partial(_scatter_kernel, n_row, n_col), out.reshape(n_img, hh, ww, n_ch),
                         latent.shape, n_dev, 1)

    spec_x = P('dp', 'row', 'col', None)
    return jax.shard_map(run_stage, mesh=mesh, in_specs=(spec_x, P('dp', None), P(), P(), P(), P(), P()), out_specs=spec_x, check_vma=False)
```

time: 1700 us -> 270 us (0.16)
  waiting for transfers between devices: 706 us -> 0 us
  matrix products: 362 us -> 0 us
  local copies, waits for them, and re-layouts: 288 us -> 3.31 us
  Pallas kernels: 0 us -> 267 us
  other arithmetic: 164 us -> 0 us
  blocking collectives: 107 us -> 0 us
  starting transfers between devices: 46 us -> 0 us
    all_gather x1 -> x0, waiting for transfers between devices: 654 us -> none  [attn_block(): kv_all = lax.all_gather(qkv_loc[1:], ('row', 'col'), axis=2, tiled=True)]
    dot_general x20 -> x0, matrix products: 301 us -> none  [the longest x8 159 us: key_step(): jnp.einsum('bhqk,bkhd->bhqd', exp_logits.astype(jnp.bfloat16), val_blk, p...]
    pallas_call x0 -> x3, Pallas kernels: none -> 267 us  [the longest x1 207 us: _stage(): pl.pallas_call(functools.partial(_stage_kernel, n_col, hh, ww), grid=(n_i...]
    unnamed x26 -> x1, local copies, waits for them, and re-layouts: 146 us -> 3.31 us
    reduce_sum x19 -> x0, other arithmetic: 138 us -> none  [the longest x8 134 us: key_step(): run_sum = run_sum * rescale + jnp.sum(exp_logits, axis=-1)]
    slice x7 -> x0, local copies, waits for them, and re-layouts: 118 us -> none  [the longest x1 97.5 us: attn_block(): kv_all[1]]
    psum x5 -> x0, blocking collectives: 107 us -> none  [group_norm(): lax.psum(part_sums, ('row', 'col')) / (n_rows * n_cols * group_ch * n_dev)]
    conv_general_dilated x4 -> x0, matrix products: 60.2 us -> none  [halo_conv(): lax.conv_general_dilated(padded, kernel, (1, 1), 'VALID', dimension_numbe...]
  transfers between devices with their start and end apart: 17 -> 0, of which waited for: 15 -> 0; matrix products, arithmetic and copies ran while one was open for 0% -> 0% of each run, Pallas kernels for 0% -> 0%
where the time goes in v1:
time: 270 us
  Pallas kernels  267 us (99%)
  local copies, waits for them, and re-layouts  3.31 us (1%)
    pallas_call x1, Pallas kernels, _stage(): pl.pallas_call(functools.partial(_stage_kernel, n_col, hh, ww), grid=(n_i...  207 us
    pallas_call x2, Pallas kernels, _exchange(): pl.pallas_call(kernel, out_shape=jax.ShapeDtypeStruct(out_shape, arr.dtyp...  59.5 us

profile of v1, /device:TPU:1, one launch (start us, length us, event | category | flops | bytes accessed | tf_op | source)
XLA Modules:
  0.0 270.2 jit_solution(9511564900103917577)
XLA Ops:
  0.0 30.4 %shard_map.73 = bf16[2,16,96,384]{3,2,1,0:T(8,128)(2,1)} custom-call(bf16[16,4,48,384]{3,2,1,0:T(8,128)(2,1)} %x_ref.1), custom_call_target="tpu_custom_call" | custom-call | tf_op jit(solution)/shard_map/pallas_call | solution.py:83
  30.4 207.4 %shard_map.74 = bf16[2,1536,384]{2,1,0:T(8,128)(2,1)} custom-call(bf16[2,1536,384]{2,1,0:T(8,128)(2,1)} %bitcast.8, bf16[16,768]{1,0:T(8,128)(2,1)} %temb_ref.1, bf16[2,2,2,384]{3,2,1,0:T(2,128)(2,1)} %rnorm_ref.1, bf16[2,2,3456,384]{3,2,1,0:T(8,128)(2,1)} %bitcast.6, bf16[2,768,384]{2,1,0:T(8,128)(2,1)} %wtemb_ref.1, bf16[2,384]{1,0:T(2,128)(2,1)} %anorm_ref.1, ...), custom_call_target="tpu_custom_call" | custom-call | tf_op jit(solution)/shard_map/pallas_call | solution.py:279
  237.8 29.0 %shard_map.75 = bf16[16,4,48,384]{3,2,1,0:T(8,128)(2,1)} custom-call(bf16[2,16,96,384]{3,2,1,0:T(8,128)(2,1)} %bitcast.7), custom_call_target="tpu_custom_call" | custom-call | tf_op jit(solution)/shard_map/pallas_call | solution.py:83
  266.8 3.3 %copy.9 = bf16[16,4,48,384]{3,2,1,0:T(8,128)(2,1)} copy(bf16[16,4,48,384]{3,2,1,0:T(8,128)(2,1)} %shard_map.75) | data formatting | bytes 4718592

commit v2 on v0

v2 whole, which is shorter than its diff:
```python
import functools

import jax
import jax.numpy as jnp
from jax import lax
from jax.experimental import pallas as pl
from jax.experimental.pallas import tpu as pltpu
from jax.sharding import PartitionSpec as P

MESH = pl.DeviceIdType.MESH
GROUPS = 32
EPS = 1e-5
LOG2E = 1.4426950408889634
F32 = jnp.float32
BF16 = jnp.bfloat16
Q_TILE = 512
K_CHUNK = 256
AHEAD = 2
ROWS_PER_CHUNK = 4


def _me_and_peers(n_row, n_col):
    me_r, me_c = lax.axis_index('row'), lax.axis_index('col')
    peers = []
    for k in range(1, n_row * n_col):
        peers.append((lax.rem(me_r + k // n_col, n_row), lax.rem(me_c + k % n_col, n_col)))
    return me_r, me_c, peers


def _barrier(peers):
    sem = pltpu.get_barrier_semaphore()
    for r, c in peers:
        pl.semaphore_signal(sem, inc=1, device_id={'row': r, 'col': c}, device_id_type=MESH)
    pl.semaphore_wait(sem, len(peers))


def _dot(a, b, dims=((1,), (0,))):
    return lax.dot_general(a, b, (dims, ((), ())), preferred_element_type=F32)


def _chan_sums(v):
    return jnp.sum(v, axis=0, keepdims=True), jnp.sum(v * v, axis=0, keepdims=True)


def _group_matrix(n_ch):
    per = n_ch // GROUPS
    gi = lax.broadcasted_iota(jnp.int32, (n_ch, n_ch), 0) // per
    gj = lax.broadcasted_iota(jnp.int32, (n_ch, n_ch), 1) // per
    return jnp.where(gi == gj, 1.0, 0.0).astype(BF16)


def _moments(s1, s2, grp, count):
    n_ch = s1.shape[1]
    st = jnp.concatenate([s1, s2, jnp.zeros((6, n_ch), F32)], axis=0)
    hi = st.astype(BF16)
    r1 = st - hi.astype(F32)
    mid = r1.astype(BF16)
    lo = (r1 - mid.astype(F32)).astype(BF16)
    tot = (_dot(lo, grp) + _dot(mid, grp)) + _dot(hi, grp)
    mean = tot[0:1] / count
    var = tot[1:2] / count - mean * mean
    return mean, lax.rsqrt(var + EPS)


def _zero_sums(n_ch):
    return jnp.zeros((1, n_ch), F32), jnp.zeros((1, n_ch), F32)


class _ResBlock:
    def __init__(self, hh, ww, n_ch, rnorm_ref, wconv, act, hid, temb_s, grp_s):
        self.hh, self.ww, self.n_ch = hh, ww, n_ch
        self.rnorm_ref, self.wconv, self.act, self.hid = rnorm_ref, wconv, act, hid
        self.temb_s, self.grp_s = temb_s, grp_s
        self.chunk = ROWS_PER_CHUNK * ww
        self.n_chunks = hh // ROWS_PER_CHUNK
        self.count = float(hh * ww * (n_ch // GROUPS))

    def setup(self, temb_ref, wtemb_ref):
        te = temb_ref[...].astype(F32)
        t_act = (te * jax.nn.sigmoid(te)).astype(BF16)
        self.temb_s[...] = _dot(t_act, wtemb_ref[...])
        self.grp_s[...] = _group_matrix(self.n_ch)
        zeros = jnp.zeros((self.ww, self.act.shape[1]), BF16)
        self.act[0:self.ww, :] = zeros
        self.act[(self.hh + 1) * self.ww:(self.hh + 2) * self.ww, :] = zeros

    def fill(self, src, sums, scale, shift):
        ww, n_ch, act = self.ww, self.n_ch, self.act
        mean, inv = _moments(*sums, self.grp_s[...], self.count)
        a_mul = inv * scale.astype(F32)
        b_add = shift.astype(F32)
        col = lax.broadcasted_iota(jnp.int32, (ww, 1), 0)

        def row(i, carry):
            r0 = pl.multiple_of(i * ww, ww)
            v = src(r0, ww).astype(F32)
            u = (v - mean) * a_mul + b_add
            a = u * (0.5 * jnp.tanh(0.5 * u) + 0.5)
            left = jnp.where(col == 0, 0.0, pltpu.roll(a, 1, 0))
            right = jnp.where(col == ww - 1, 0.0, pltpu.roll(a, ww - 1, 0))
            d0 = pl.multiple_of(r0 + ww, ww)
            act[pl.ds(d0, ww), 0:n_ch] = left.astype(BF16)
            act[pl.ds(d0, ww), n_ch:2 * n_ch] = a.astype(BF16)
            act[pl.ds(d0, ww), 2 * n_ch:3 * n_ch] = right.astype(BF16)
            return carry

        lax.fori_loop(0, self.hh, row, 0)

    def conv(self, j, first_chunk, epilogue):
        chunk, ww = self.chunk, self.ww

        def body(i, sums):
            k = lax.rem(i + first_chunk, self.n_chunks)
            r0 = pl.multiple_of(k * chunk, chunk)
            lhs = jnp.concatenate(
                [self.act[pl.ds(pl.multiple_of(r0 + dy * ww, ww), chunk), :] for dy in range(3)], axis=1)
            out = epilogue(k, r0, _dot(lhs, self.wconv[j]))
            d1, d2 = _chan_sums(out.astype(F32))
            return sums[0] + d1, sums[1] + d2

        return lax.fori_loop(0, self.n_chunks, body, _zero_sums(self.n_ch))

    def input_sums(self, src):
        def body(i, sums):
            d1, d2 = _chan_sums(src(pl.multiple_of(i * self.chunk, self.chunk), self.chunk).astype(F32))
            return sums[0] + d1, sums[1] + d2

        return lax.fori_loop(0, self.n_chunks, body, _zero_sums(self.n_ch))

    def run(self, src, img, wait_weight, first_chunk, dst):
        chunk, hid, rnorm_ref = self.chunk, self.hid, self.rnorm_ref
        self.fill(src, self.input_sums(src), rnorm_ref[0, 0:1], rnorm_ref[0, 1:2])
        t_row = self.temb_s[pl.ds(img, 1), :]

        def first(k, r0, acc):
            out = (acc + t_row).astype(BF16)
            hid[pl.ds(r0, chunk), :] = out
            return out

        wait_weight(0)
        sums = self.conv(0, 0, first)
        self.fill(lambda r0, n: hid[pl.ds(r0, n), :], sums, rnorm_ref[1, 0:1], rnorm_ref[1, 1:2])

        def second(k, r0, acc):
            out = (src(r0, chunk).astype(F32) + acc).astype(BF16)
            dst(k, r0, out)
            return out

        wait_weight(1)
        self.conv(1, first_chunk, second)


def _weight_copies(r, conv_hbm, wconv, wtemb_hbm, wtemb, sem):
    convs = [pltpu.make_async_copy(conv_hbm.at[r, i], wconv.at[i], sem.at[i]) for i in range(2)]
    return convs, pltpu.make_async_copy(wtemb_hbm.at[r], wtemb, sem.at[2])


def _first_kernel(n_row, n_col, lat_ref, temb_ref, rnorm_ref, conv_hbm, wtemb_hbm, o_ref,
                  xv, wconv, wtemb, act, hid, temb_s, grp_s, wsem, send_sem, recv_sem, loc_sem):
    me_r, me_c, peers = _me_and_peers(n_row, n_col)
    me = me_r * n_col + me_c
    n_img, hh, ww, n_ch = xv.shape
    bh, bw = hh // n_row, ww // n_col
    weights, temb_copy = _weight_copies(0, conv_hbm, wconv, wtemb_hbm, wtemb, wsem)
    for w in [temb_copy, *weights]:
        w.start()

    def place(s):
        return xv.at[s, pl.ds(me_r * bh, bh), pl.ds(pl.multiple_of(me_c * bw, bw), bw), :]

    def copy(s, k):
        r, c = peers[k]
        return pltpu.make_async_remote_copy(
            lat_ref.at[(r * n_col + c) * n_img + s], place(s), send_sem.at[s, k], recv_sem.at[s, k],
            device_id={'row': r, 'col': c}, device_id_type=MESH)

    def own(s):
        return pltpu.make_async_copy(lat_ref.at[me * n_img + s], place(s), loc_sem.at[s])

    _barrier(peers)
    for s in range(n_img):
        for k in range(len(peers)):
            copy(s, k).start()
        own(s).start()

    blk = _ResBlock(hh, ww, n_ch, rnorm_ref.at[0], wconv, act, hid, temb_s, grp_s)
    temb_copy.wait()
    blk.setup(temb_ref, wtemb)

    def image(s, carry):
        for k in range(len(peers)):
            copy(s, k).wait_recv()
        own(s).wait()

        def src(r0, n):
            return xv[s, pl.ds(r0 // ww, n // ww)].reshape(n, n_ch)

        def dst(k, r0, v):
            o_ref[s, pl.ds(r0, blk.chunk), :] = v

        def wait_weight(j):
            @pl.when(s == 0)
            def _():
                weights[j].wait()

        blk.run(src, me * n_img + s, wait_weight, 0, dst)
        return carry

    lax.fori_loop(0, n_img, image, 0)
    for s in range(n_img):
        for k in range(len(peers)):
            copy(s, k).wait_send()


def _last_kernel(n_row, n_col, x_ref, temb_ref, rnorm_ref, conv_hbm, wtemb_hbm, o_ref,
                 yv, wconv, wtemb, act, hid, temb_s, grp_s, wsem, send_sem, recv_sem, loc_sem):
    me_r, me_c, peers = _me_and_peers(n_row, n_col)
    me = me_r * n_col + me_c
    n_img, hh, ww, n_ch = yv.shape
    bh, bw = hh // n_row, ww // n_col
    weights, temb_copy = _weight_copies(1, conv_hbm, wconv, wtemb_hbm, wtemb, wsem)
    for w in [temb_copy, *weights]:
        w.start()
    blk = _ResBlock(hh, ww, n_ch, rnorm_ref.at[1], wconv, act, hid, temb_s, grp_s)
    temb_copy.wait()
    blk.setup(temb_ref, wtemb)
    _barrier(peers)
    first_chunk = lax.rem(me_r + n_row // 2, n_row) // (n_row // 2) * (n_row // 2)

    def block(s, k, c):
        return yv.at[s, pl.ds(k * bh, bh), pl.ds(pl.multiple_of(c * bw, bw), bw), :]

    def rel(k, c):
        return lax.rem(k - me_r + n_row, n_row) * n_col + lax.rem(c - me_c + n_col, n_col)

    def copy(s, k, c):
        return pltpu.make_async_remote_copy(
            block(s, k, c), o_ref.at[me * n_img + s], send_sem.at[s, rel(k, c)], recv_sem.at[s, rel(k, c)],
            device_id={'row': k, 'col': c}, device_id_type=MESH)

    def own(s):
        return pltpu.make_async_copy(block(s, me_r, me_c), o_ref.at[me * n_img + s], loc_sem.at[s])

    def image(s, carry):
        def src(r0, n):
            return x_ref[s, pl.ds(r0, n), :]

        def dst(k, r0, v):
            yv[s, pl.ds(r0 // ww, ROWS_PER_CHUNK)] = v.reshape(ROWS_PER_CHUNK, ww, n_ch)
            for d in range(n_col):
                c = lax.rem(me_c + 1 + d, n_col)
                remote = (k != me_r) | (c != me_c)

                @pl.when(remote)
                def _():
                    copy(s, k, c).start()

                @pl.when(jnp.logical_not(remote))
                def _():
                    own(s).start()

        def wait_weight(j):
            @pl.when(s == 0)
            def _():
                weights[j].wait()

        blk.run(src, me * n_img + s, wait_weight, first_chunk, dst)
        return carry

    lax.fori_loop(0, n_img, image, 0)
    for s in range(n_img):
        for r, c in peers:
            copy(s, r, c).wait()
        own(s).wait()


def _attn_kernel(x_ref, anorm_ref, proj_ref, o_ref, grp_s, k_buf, q_buf, v_buf, ot_buf):
    n_pos, n_ch = x_ref.shape[1:]
    count = float(n_pos * (n_ch // GROUPS))
    head_dim = 32
    n_heads = n_ch // head_dim
    per_blk = 128 // head_dim
    scale = LOG2E * head_dim ** -0.5

    @pl.when(pl.program_id(0) == 0)
    def _():
        grp_s[...] = _group_matrix(n_ch)

    def in_sums(i, sums):
        d1, d2 = _chan_sums(x_ref[0, pl.ds(pl.multiple_of(i * 256, 256), 256), :].astype(F32))
        return sums[0] + d1, sums[1] + d2

    sums = lax.fori_loop(0, n_pos // 256, in_sums, _zero_sums(n_ch))
    mean, inv = _moments(*sums, grp_s[...], count)
    a_mul = inv * anorm_ref[0:1].astype(F32)
    b_add = anorm_ref[1:2].astype(F32)
    head_rows = jnp.where(lax.broadcasted_iota(jnp.int32, (16, n_ch), 0)
                          == lax.broadcasted_iota(jnp.int32, (16, n_ch), 1) // head_dim, 1.0, 0.0).astype(BF16)

    def project(i, tops):
        r0 = pl.multiple_of(i * 256, 256)
        g = ((x_ref[0, pl.ds(r0, 256), :].astype(F32) - mean) * a_mul + b_add).astype(BF16)
        q = _dot(proj_ref[0], g, ((1,), (1,))).astype(BF16)
        v = _dot(proj_ref[2], g, ((1,), (1,))).astype(BF16)
        k = _dot(g, proj_ref[1], ((1,), (1,))).astype(BF16)
        q_buf[:, pl.ds(r0, 256)] = q
        v_buf[:, pl.ds(r0, 256)] = v
        k_buf[pl.ds(r0, 256), :] = k
        q2 = _dot(head_rows, (q.astype(F32) * q.astype(F32)).astype(BF16))
        k2 = _dot(head_rows, (k.astype(F32) * k.astype(F32)).astype(BF16), ((1,), (1,)))
        v_top = jnp.max(jnp.abs(v.astype(F32)), axis=0, keepdims=True)
        return jnp.maximum(tops[0], q2), jnp.maximum(tops[1], k2), jnp.maximum(tops[2], v_top)

    tops = lax.fori_loop(0, n_pos // 256, project,
                         (jnp.zeros((16, 256), F32), jnp.zeros((16, 256), F32), jnp.zeros((1, 256), F32)))
    small = (jnp.max(tops[0]) * scale * scale * jnp.max(tops[1]) < 1600.0) & (jnp.max(tops[2]) < 2.0 ** 60)

    @pl.when(small)
    def _():
        rh = lax.broadcasted_iota(jnp.int32, (128, Q_TILE), 0) // head_dim
        n_kc = n_pos // K_CHUNK

        def heads(b, carry):
            b0 = pl.multiple_of(b * 128, 128)
            tiles = [(j, t * Q_TILE) for j in range(per_blk) for t in range(n_pos // Q_TILE)]
            steps = [(tile, c) for tile in tiles for c in range(n_kc)]
            masked = {}

            def score(step):
                tile, c = step
                if tile not in masked:
                    j, q0 = tile
                    masked[tile] = jnp.where(rh == j, q_buf[pl.ds(b0, 128), q0:q0 + Q_TILE], 0)
                return _dot(k_buf[c * K_CHUNK:(c + 1) * K_CHUNK, pl.ds(b0, 128)], masked[tile])

            pending = [score(s) for s in steps[:AHEAD]]
            tot = out = None
            for n, ((j, q0), c) in enumerate(steps):
                if n + AHEAD < len(steps):
                    pending.append(score(steps[n + AHEAD]))
                p = jnp.exp2(pending.pop(0) * scale)
                h0 = pl.multiple_of(b0 + j * head_dim, head_dim)
                part = jnp.sum(p.reshape(K_CHUNK // 8, 8, Q_TILE), axis=0)
                pv = _dot(v_buf[pl.ds(h0, head_dim), c * K_CHUNK:(c + 1) * K_CHUNK], p.astype(BF16))
                tot, out = (part, pv) if c == 0 else (tot + part, out + pv)
                if c == n_kc - 1:
                    res = out / jnp.sum(tot, axis=0, keepdims=True)
                    ot_buf[pl.ds(h0, head_dim), q0:q0 + Q_TILE] = res.astype(BF16)
            return carry

        lax.fori_loop(0, n_ch // 128, heads, 0)

    @pl.when(jnp.logical_not(small))
    def _():
        rh = lax.broadcasted_iota(jnp.int32, (128, 256), 0) // head_dim
        n_tiles = n_pos // 256

        def tile(i, carry):
            h = i // n_tiles
            q0 = pl.multiple_of((i % n_tiles) * 256, 256)
            b0 = pl.multiple_of((h // per_blk) * 128, 128)
            h0 = pl.multiple_of(h * head_dim, head_dim)
            qm = jnp.where(rh == h % per_blk, q_buf[pl.ds(b0, 128), pl.ds(q0, 256)], 0)
            s = _dot(k_buf[:, pl.ds(b0, 128)], qm)
            p = jnp.exp2((s - jnp.max(s, axis=0, keepdims=True)) * scale)
            o = _dot(v_buf[pl.ds(h0, head_dim), :], p.astype(BF16))
            ot_buf[pl.ds(h0, head_dim), pl.ds(q0, 256)] = (o / jnp.sum(p, axis=0, keepdims=True)).astype(BF16)
            return carry

        lax.fori_loop(0, n_heads * n_tiles, tile, 0)

    def out_proj(i, carry):
        r0 = pl.multiple_of(i * 256, 256)
        acc = _dot(ot_buf[:, pl.ds(r0, 256)], proj_ref[3], ((0,), (0,)))
        o_ref[0, pl.ds(r0, 256), :] = (x_ref[0, pl.ds(r0, 256), :].astype(F32) + acc).astype(BF16)
        return carry

    lax.fori_loop(0, n_pos // 256, out_proj, 0)


VMEM_LIMIT = 60 * 1024 * 1024


def _res_scratch(hh, ww, n_ch, n_batch, n_temb, n_img, n_dev):
    return [
        pltpu.VMEM((n_img, hh, ww, n_ch), BF16),
        pltpu.VMEM((2, 9 * n_ch, n_ch), BF16),
        pltpu.VMEM((n_temb, n_ch), BF16),
        pltpu.VMEM(((hh + 2) * ww, 3 * n_ch), BF16),
        pltpu.VMEM((hh * ww, n_ch), BF16),
        pltpu.VMEM((n_batch, n_ch), F32),
        pltpu.VMEM((n_ch, n_ch), BF16),
        pltpu.SemaphoreType.DMA((3,)),
        pltpu.SemaphoreType.DMA((n_img, n_dev)),
        pltpu.SemaphoreType.DMA((n_img, n_dev)),
        pltpu.SemaphoreType.DMA((n_img,)),
    ]


def solution(mesh):
    n_row, n_col = mesh.shape['row'], mesh.shape['col']
    n_dev = n_row * n_col
    vmem, hbm = pl.BlockSpec(memory_space=pltpu.VMEM), pl.BlockSpec(memory_space=pl.ANY)

    def run_stage(latent, t_emb, res_norm, res_conv, res_temb, attn_norm, attn_proj):
        n_batch, bh, bw, n_ch = latent.shape
        hh, ww = bh * n_row, bw * n_col
        n_pos, n_img = hh * ww, n_batch // n_dev
        proj = jnp.transpose(attn_proj, (0, 1, 3, 2)).reshape(4, n_ch, n_ch)
        conv_w = res_conv.reshape(2, 2, 9 * n_ch, n_ch)
        scratch = _res_scratch(hh, ww, n_ch, n_batch, t_emb.shape[1], n_img, n_dev)

        x1 = pl.pallas_call(
            functools.partial(_first_kernel, n_row, n_col),
            out_shape=jax.ShapeDtypeStruct((n_img, n_pos, n_ch), BF16),
            in_specs=[hbm, vmem, vmem, hbm, hbm],
            out_specs=vmem,
            scratch_shapes=scratch,
            compiler_params=pltpu.CompilerParams(collective_id=0, has_side_effects=True, vmem_limit_bytes=VMEM_LIMIT),
        )(latent, t_emb, res_norm, conv_w, res_temb)

        def whole(a):
            return pl.BlockSpec(a.shape, lambda i, nd=a.ndim: (0,) * nd, pipeline_mode=pl.Buffered(1))

        img_spec = pl.BlockSpec((1, n_pos, n_ch), lambda i: (i, 0, 0))
        x2 = pl.pallas_call(
            _attn_kernel,
            grid=(n_img,),
            out_shape=jax.ShapeDtypeStruct((n_img, n_pos, n_ch), BF16),
            in_specs=[img_spec, whole(attn_norm), whole(proj)],
            out_specs=img_spec,
            scratch_shapes=[
                pltpu.VMEM((n_ch, n_ch), BF16),
                pltpu.VMEM((n_pos, n_ch), BF16),
                pltpu.VMEM((n_ch, n_pos), BF16),
                pltpu.VMEM((n_ch, n_pos), BF16),
                pltpu.VMEM((n_ch, n_pos), BF16),
            ],
            compiler_params=pltpu.CompilerParams(dimension_semantics=("arbitrary",), vmem_limit_bytes=VMEM_LIMIT),
        )(x1, attn_norm, proj)

        return pl.pallas_call(
            functools.partial(_last_kernel, n_row, n_col),
            out_shape=jax.ShapeDtypeStruct(latent.shape, BF16),
            in_specs=[vmem, vmem, vmem, hbm, hbm],
            out_specs=hbm,
            scratch_shapes=scratch,
            compiler_params=pltpu.CompilerParams(collective_id=1, has_side_effects=True, vmem_limit_bytes=VMEM_LIMIT),
        )(x2, t_emb, res_norm, conv_w, res_temb)

    spec_x = P('dp', 'row', 'col', None)
    return jax.shard_map(run_stage, mesh=mesh, in_specs=(spec_x, P('dp', None), P(), P(), P(), P(), P()), out_specs=spec_x, check_vma=False)
```

time: 1700 us -> 253 us (0.15)
  waiting for transfers between devices: 706 us -> 0 us
  matrix products: 362 us -> 0 us
  local copies, waits for them, and re-layouts: 288 us -> 3.31 us
  Pallas kernels: 0 us -> 250 us
  other arithmetic: 164 us -> 0 us
  blocking collectives: 107 us -> 0 us
  starting transfers between devices: 46 us -> 0 us
    all_gather x1 -> x0, waiting for transfers between devices: 654 us -> none  [attn_block(): kv_all = lax.all_gather(qkv_loc[1:], ('row', 'col'), axis=2, tiled=True)]
    dot_general x20 -> x0, matrix products: 301 us -> none  [the longest x8 159 us: key_step(): jnp.einsum('bhqk,bkhd->bhqd', exp_logits.astype(jnp.bfloat16), val_blk, p...]
    pallas_call x0 -> x3, Pallas kernels: none -> 250 us  [the longest x1 149 us: run_stage(): pl.pallas_call(_attn_kernel, grid=(n_img,), out_shape=jax.ShapeDtypeStruc...]
    unnamed x26 -> x1, local copies, waits for them, and re-layouts: 146 us -> 3.31 us
    reduce_sum x19 -> x0, other arithmetic: 138 us -> none  [the longest x8 134 us: key_step(): run_sum = run_sum * rescale + jnp.sum(exp_logits, axis=-1)]
    slice x7 -> x0, local copies, waits for them, and re-layouts: 118 us -> none  [the longest x1 97.5 us: attn_block(): kv_all[1]]
    psum x5 -> x0, blocking collectives: 107 us -> none  [group_norm(): lax.psum(part_sums, ('row', 'col')) / (n_rows * n_cols * group_ch * n_dev)]
    conv_general_dilated x4 -> x0, matrix products: 60.2 us -> none  [halo_conv(): lax.conv_general_dilated(padded, kernel, (1, 1), 'VALID', dimension_numbe...]
  transfers between devices with their start and end apart: 17 -> 0, of which waited for: 15 -> 0; matrix products, arithmetic and copies ran while one was open for 0% -> 0% of each run, Pallas kernels for 0% -> 0%
where the time goes in v2:
time: 253 us
  Pallas kernels  250 us (99%)
  local copies, waits for them, and re-layouts  3.31 us (1%)
    pallas_call x1, Pallas kernels, run_stage(): pl.pallas_call(_attn_kernel, grid=(n_img,), out_shape=jax.ShapeDtypeStruc...  149 us
    pallas_call x1, Pallas kernels, run_stage(): pl.pallas_call(functools.partial(_first_kernel, n_row, n_col), out_shape=...  53.4 us
    pallas_call x1, Pallas kernels, run_stage(): pl.pallas_call(functools.partial(_last_kernel, n_row, n_col), out_shape=j...  47.2 us

profile of v2, /device:TPU:1, one launch (start us, length us, event | category | flops | bytes accessed | tf_op | source)
XLA Modules:
  0.0 253.0 jit_solution(12292121332828633636)
XLA Ops:
  0.0 53.4 %shard_map.73.x_ref = bf16[2,1536,384]{2,1,0:T(8,128)(2,1)} custom-call(bf16[16,4,48,384]{3,2,1,0:T(8,128)(2,1)} %lat_ref.1, bf16[16,768]{1,0:T(8,128)(2,1)} %temb_ref.3, bf16[2,2,2,384]{3,2,1,0:T(2,128)(2,1)} %rnorm_ref.3, bf16[2,2,3456,384]{3,2,1,0:T(8,128)(2,1)} %bitcast.4, bf16[2,768,384]{2,1,0:T(8,128)(2,1)} %wtemb_hbm.3), custom_call_target="tpu_custom_call" | custom-call | tf_op jit(solution)/shard_map/pallas_call | solution.py:413
  53.4 149.1 %shard_map.74.x_ref = bf16[2,1536,384]{2,1,0:T(8,128)(2,1)} custom-call(bf16[2,1536,384]{2,1,0:T(8,128)(2,1)} %shard_map.73.x_ref, bf16[2,384]{1,0:T(2,128)(2,1)} %anorm_ref.1, bf16[4,384,384]{2,1,0:T(8,128)(2,1)} %bitcast.6), custom_call_target="tpu_custom_call" | custom-call | tf_op jit(solution)/shard_map/pallas_call | solution.py:426
  202.5 47.2 %shard_map.75 = bf16[16,4,48,384]{3,2,1,0:T(8,128)(2,1)} custom-call(bf16[2,1536,384]{2,1,0:T(8,128)(2,1)} %shard_map.74.x_ref, bf16[16,768]{1,0:T(8,128)(2,1)} %temb_ref.3, bf16[2,2,2,384]{3,2,1,0:T(2,128)(2,1)} %rnorm_ref.3, bf16[2,2,3456,384]{3,2,1,0:T(8,128)(2,1)} %bitcast.5, bf16[2,768,384]{2,1,0:T(8,128)(2,1)} %wtemb_hbm.3), custom_call_target="tpu_custom_call" | custom-call | tf_op jit(solution)/shard_map/pallas_call | solution.py:442
  249.7 3.3 %copy.9 = bf16[16,4,48,384]{3,2,1,0:T(8,128)(2,1)} copy(bf16[16,4,48,384]{3,2,1,0:T(8,128)(2,1)} %shard_map.75) | data formatting | bytes 4718592

commit v3 on v2

--- a/solution.py
+++ b/solution.py
@@ -313,7 +313,11 @@
 
     tops = lax.fori_loop(0, n_pos // 256, project,
                          (jnp.zeros((16, 256), F32), jnp.zeros((16, 256), F32), jnp.zeros((1, 256), F32)))
-    small = (jnp.max(tops[0]) * scale * scale * jnp.max(tops[1]) < 1600.0) & (jnp.max(tops[2]) < 2.0 ** 60)
+    q_top = jnp.max(tops[0], axis=1, keepdims=True)
+    k_top = jnp.max(tops[1], axis=1, keepdims=True)
+    top2 = jnp.max(q_top * k_top) * (scale * scale)
+    v_max = jnp.max(tops[2])
+    small = ((top2 < 96.0 ** 2) & (v_max < 2.0 ** 20)) | ((top2 < 108.0 ** 2) & (v_max < 2.0 ** 8))
 
     @pl.when(small)
     def _():

time: 253 us -> 210 us (0.83)
  Pallas kernels: 250 us -> 206 us
    pallas_call x1, Pallas kernels: 149 us -> 62.7 us  [run_stage(): pl.pallas_call(_attn_kernel, grid=(n_img,), out_shape=jax.ShapeDtypeStruc...]
    pallas_call x1, Pallas kernels: 47.2 us -> 90.3 us  [run_stage(): pl.pallas_call(functools.partial(_last_kernel, n_row, n_col), out_shape=j...]
where the time goes in v3:
time: 210 us
  Pallas kernels  206 us (98%)
  local copies, waits for them, and re-layouts  3.31 us (2%)
    pallas_call x1, Pallas kernels, run_stage(): pl.pallas_call(functools.partial(_last_kernel, n_row, n_col), out_shape=j...  90.3 us
    pallas_call x1, Pallas kernels, run_stage(): pl.pallas_call(_attn_kernel, grid=(n_img,), out_shape=jax.ShapeDtypeStruc...  62.7 us
    pallas_call x1, Pallas kernels, run_stage(): pl.pallas_call(functools.partial(_first_kernel, n_row, n_col), out_shape=...  53.4 us

profile of v3, /device:TPU:1, one launch (start us, length us, event | category | flops | bytes accessed | tf_op | source)
XLA Modules:
  0.0 209.7 jit_solution(8301318337861547840)
XLA Ops:
  0.0 53.4 %shard_map.73.x_ref = bf16[2,1536,384]{2,1,0:T(8,128)(2,1)} custom-call(bf16[16,4,48,384]{3,2,1,0:T(8,128)(2,1)} %lat_ref.1, bf16[16,768]{1,0:T(8,128)(2,1)} %temb_ref.3, bf16[2,2,2,384]{3,2,1,0:T(2,128)(2,1)} %rnorm_ref.3, bf16[2,2,3456,384]{3,2,1,0:T(8,128)(2,1)} %bitcast.4, bf16[2,768,384]{2,1,0:T(8,128)(2,1)} %wtemb_hbm.3), custom_call_target="tpu_custom_call" | custom-call | tf_op jit(solution)/shard_map/pallas_call | solution.py:417
  53.4 62.7 %shard_map.74.x_ref = bf16[2,1536,384]{2,1,0:T(8,128)(2,1)} custom-call(bf16[2,1536,384]{2,1,0:T(8,128)(2,1)} %shard_map.73.x_ref, bf16[2,384]{1,0:T(2,128)(2,1)} %anorm_ref.1, bf16[4,384,384]{2,1,0:T(8,128)(2,1)} %bitcast.6), custom_call_target="tpu_custom_call" | custom-call | tf_op jit(solution)/shard_map/pallas_call | solution.py:430
  116.0 90.3 %shard_map.75 = bf16[16,4,48,384]{3,2,1,0:T(8,128)(2,1)} custom-call(bf16[2,1536,384]{2,1,0:T(8,128)(2,1)} %shard_map.74.x_ref, bf16[16,768]{1,0:T(8,128)(2,1)} %temb_ref.3, bf16[2,2,2,384]{3,2,1,0:T(2,128)(2,1)} %rnorm_ref.3, bf16[2,2,3456,384]{3,2,1,0:T(8,128)(2,1)} %bitcast.5, bf16[2,768,384]{2,1,0:T(8,128)(2,1)} %wtemb_hbm.3), custom_call_target="tpu_custom_call" | custom-call | tf_op jit(solution)/shard_map/pallas_call | solution.py:446
  206.4 3.3 %copy.9 = bf16[16,4,48,384]{3,2,1,0:T(8,128)(2,1)} copy(bf16[16,4,48,384]{3,2,1,0:T(8,128)(2,1)} %shard_map.75) | data formatting | bytes 4718592
